TPU v7x, 32 devices: a whole 2x2x4 slice. The times are simulated.
32 devices in a mesh: row: 16 (over z, x, core), col: 2 (over y).
Axes of the slice: x: 2, y: 2, z: 4, core: 2. Of those that a mesh axis runs over, the one named last changes fastest.
Arguments:
- pivots: int32 [256], replicated, may hold values from 0 to 4095, as said below
- panel: float32 [4096, 256], P(('row', 'col')), may hold values from -6 to 6
- prior: bfloat16 [4096, 3072], P(('row', 'col')), may hold values from -0.796875 to 0.796875
- finished: bfloat16 [4096, 256], P(('row', 'col')), may hold values from -6 to 6
- pairs: int32 [4096], replicated, may hold values from 0 to 639999, as said below
- occupied: bfloat16 [800, 120], replicated, may hold values from -0.21875 to 0.21875
Outputs:
- updated: float32 [4096, 256], P(('row', 'col'))
- halves: float32 [256, 120, 800], P(('row', 'col'))
Inputs may be any that keep to these rules, and one draw needn't show every extreme that they name: `pivots`: distinct rows; at most 16 of them lie among the rows of one device (aligned blocks of 128 rows), and one device holds exactly 16. `pairs`: each value a * 800 + b with 0 <= b <= a < 800; all distinct and increasing.
All inputs are finite; a program needn't handle non-finite values.
Results may differ from a plain program's by a relative error of at most 0.0003.
Values may be sent and summed in bfloat16 or wider, within the bound.
A program may use at most 64 MiB of HBM per device.

v0:
```python
import jax
import jax.numpy as jnp
from jax import lax
from jax.sharding import PartitionSpec as P


def half_transform(received, pair_ids, occupied):
    orbitals = occupied.shape[0]
    pair_count = received.shape[0]
    vector_count = received.shape[1]
    first_ao = pair_ids // orbitals
    second_ao = pair_ids % orbitals
    off_diag = first_ao != second_ao
    occ_first = jnp.take(occupied, first_ao, axis=0)
    occ_second = jnp.where(
        off_diag[:, None], jnp.take(occupied, second_ao, axis=0), jnp.zeros((), jnp.bfloat16)
    )
    coeffs = jnp.concatenate([occ_first, occ_second], axis=0)
    targets = jnp.concatenate([second_ao, first_ao], axis=0).astype(jnp.int32)
    entries = jnp.concatenate([received, received], axis=0)
    doubled = 2 * pair_count
    wanted = min(doubled, max(1024, doubled // 8))
    block_rows = wanted
    for candidate in range(wanted, 0, -1):
        if doubled % candidate == 0:
            block_rows = candidate
            break
    columns = jnp.arange(orbitals, dtype=jnp.int32)

    def one_block(block_index, accumulated):
        start = block_index * block_rows
        coeff_block = lax.dynamic_slice_in_dim(coeffs, start, block_rows, 0)
        target_block = lax.dynamic_slice_in_dim(targets, start, block_rows, 0)
        entry_block = lax.dynamic_slice_in_dim(entries, start, block_rows, 0)
        matches = target_block[:, None] == columns[None, :]
        spread = jnp.where(
            matches[None, :, :], entry_block.T[:, :, None], jnp.zeros((), jnp.bfloat16)
        )
        return accumulated + jnp.einsum(
            "pi,vpm->vim", coeff_block, spread, preferred_element_type=jnp.float32
        )

    initial = jnp.zeros((vector_count, occupied.shape[1], orbitals), jnp.float32)
    return lax.fori_loop(0, doubled // block_rows, one_block, initial)


def per_device(pivots, panel, prior, finished, pairs, occupied):
    rows_dev = prior.shape[0]
    row_count = lax.axis_size("row")
    col_count = lax.axis_size("col")
    devices = row_count * col_count
    own_index = lax.axis_index("row") * col_count + lax.axis_index("col")
    owner = pivots // rows_dev
    local_rows = pivots % rows_dev
    owned = owner == own_index
    piv_count = pivots.shape[0]
    slot_cap = max(2, 2 * piv_count // devices)
    counter = jnp.arange(piv_count, dtype=jnp.int32)
    earlier = counter[None, :] < counter[:, None]
    same_owner = owner[None, :] == owner[:, None]
    earlier_count = jnp.sum(earlier & same_owner, axis=1).astype(jnp.int32)
    slot_hit = owned[None, :] & (
        earlier_count[None, :] == jnp.arange(slot_cap, dtype=jnp.int32)[:, None]
    )
    offsets = jnp.sum(jnp.where(slot_hit, local_rows[None, :], 0), axis=1).astype(jnp.int32)
    slot_rows = jnp.take(prior, offsets, axis=0)
    gathered = lax.all_gather(slot_rows, ("row", "col"), axis=0, tiled=True)
    pivot_rows = jnp.take(gathered, owner * slot_cap + earlier_count, axis=0)
    updated = panel - lax.dot_general(
        prior, pivot_rows, (((1,), (1,)), ((), ())), preferred_element_type=jnp.float32
    )
    by_device = pairs.reshape(row_count, col_count, rows_dev)
    col_pairs = lax.dynamic_slice_in_dim(by_device, lax.axis_index("col"), 1, 1).reshape(-1)
    grouped = finished.reshape(rows_dev, row_count, finished.shape[1] // row_count)
    received = lax.all_to_all(grouped, "row", split_axis=1, concat_axis=0, tiled=True)
    partials = half_transform(
        received.reshape(received.shape[0], received.shape[2]), col_pairs, occupied
    )
    halves = lax.psum_scatter(partials, "col", scatter_dimension=0, tiled=True)
    return (updated, halves)


def solution(mesh):
    return jax.shard_map(
        per_device,
        mesh=mesh,
        in_specs=(
            P(),
            P(("row", "col"), None),
            P(("row", "col"), None),
            P(("row", "col"), None),
            P(),
            P(),
        ),
        out_specs=(P(("row", "col"), None), P(("row", "col"), None, None)),
        check_vma=False,
    )
```

profile of v0, /device:TPU:0, one launch (start us, length us, event | category | flops | bytes accessed | tf_op | source)
XLA Modules:
  0.0 169.9 jit_solution(15981918828450987510)
XLA Ops:
  8.0 1.7 copy.22
  9.7 7.4 %all-to-all-start = ((bf16[128,16,16]{0,2,1:T(8,128)(2,1)}), bf16[128,16,16]{0,2,1:T(8,128)(2,1)S(1)}, u32[]{:S(2)}, u32[]{:S(2)}) async-start(bf16[128,16,16]{0,2,1:T(8,128)(2,1)} %bitcast.6), calls=%async_computation | async-start | bytes 131072 | tf_op jit(solution)/shard_map/all_to_all | solution.py:75
  17.1 0.7 and_select_fusion
  17.8 0.7 broadcast_compare_fusion.1
  18.5 0.2 convert_reduce_fusion
  18.7 0.1 select_reduce_fusion
  18.9 0.6 gather_fusion
  19.5 0.7 broadcast_select_fusion.1
  20.2 0.0 reduce-scatter.2.cloned.1.call-start
  20.3 0.8 broadcast_remainder_fusion
  21.0 0.8 compare_reduce_fusion
  21.9 6.2 %gather_fusion.3 = bf16[2048,120]{1,0:T(8,128)(2,1)S(1)} fusion(bf16[800,120]{1,0:T(8,128)(2,1)S(1)} %copy-done.1, s32[2048]{0:T(1024)S(1)} %get-tuple-element.181), kind=kCustom, calls=%fused_computation.1.clone | custom fusion | bytes 991232 | tf_op jit(solution)/shard_map/jit(_take)/gather | solution.py:16
  28.1 6.2 %gather_fusion.2 = bf16[2048,120]{1,0:T(8,128)(2,1)S(1)} fusion(bf16[800,120]{1,0:T(8,128)(2,1)S(1)} %copy-done.1, s32[2048]{0:T(1024)S(1)} %fusion.25), kind=kCustom, calls=%fused_computation.clone | custom fusion | bytes 991232 | tf_op jit(solution)/shard_map/jit(_take)/gather | solution.py:14
  34.3 0.3 broadcast_select_fusion
  34.6 1.5 select_select_fusion
  36.1 0.2 pad_maximum_fusion
  36.3 0.5 copy.24
  36.9 44.1 %while.14 = (s32[]{:T(128)}, f32[16,120,800]{1,2,0:T(8,128)}, s32[4096]{0:T(1024)S(1)}, bf16[4096,16]{0,1:T(8,128)(2,1)S(1)}, bf16[4096,120]{0,1:T(8,128)(2,1)S(...) while((s32[]{:T(128)}, f32[16,120,800]{1,2,0:T(8,128)}, s32[4096]{0:T(1024)S(1)}, ...), condition=%wide.region_3.5_spmd.clone, body=%wide.region_2.4_spmd.clone.sunk | while | flops 3162726400 | bytes 14282913 | solution.py:44
  37.0 0.6 iota_compare_fusion.4
  37.6 9.0 %bitcast_add_fusion.2 = f32[16,120,800]{1,2,0:T(8,128)} fusion(f32[16,120,800]{1,2,0:T(8,128)} %get-tuple-element.224, pred[]{:T(512)S(6)} %compare.6, pred[1024,800]{0,1:T(8,128)(4,1)S(1)} %iota_compare_fusion.4, bf16[16,1024]{1,0:T(8,128)(2,1)S(1)} %dynamic-slice_bitcast_fusion.2, bf16[4096,120]{0,1:T(8,128)(2,1)S(1)} %get-tuple-element.236, ...), kind=kOutput, calls=%fused_computation.10.clone.1 | convolution fusion | flops 3161907200 | bytes 13385733 | tf_op jit(solution)/shard_map/while/body/eval_jaxpr/pi,vpm->vim/dot_general | solution.py:39
  46.6 0.6 iota_compare_fusion.4
  47.2 10.9 %bitcast_add_fusion.2 = f32[16,120,800]{1,2,0:T(8,128)} fusion(f32[16,120,800]{1,2,0:T(8,128)} %get-tuple-element.224, pred[]{:T(512)S(6)} %compare.6, pred[1024,800]{0,1:T(8,128)(4,1)S(1)} %iota_compare_fusion.4, bf16[16,1024]{1,0:T(8,128)(2,1)S(1)} %dynamic-slice_bitcast_fusion.2, bf16[4096,120]{0,1:T(8,128)(2,1)S(1)} %get-tuple-element.236, ...), kind=kOutput, calls=%fused_computation.10.clone.1 | convolution fusion | flops 3161907200 | bytes 13385733 | tf_op jit(solution)/shard_map/while/body/eval_jaxpr/pi,vpm->vim/dot_general | solution.py:39
  58.1 0.6 iota_compare_fusion.4
  58.7 10.9 %bitcast_add_fusion.2 = f32[16,120,800]{1,2,0:T(8,128)} fusion(f32[16,120,800]{1,2,0:T(8,128)} %get-tuple-element.224, pred[]{:T(512)S(6)} %compare.6, pred[1024,800]{0,1:T(8,128)(4,1)S(1)} %iota_compare_fusion.4, bf16[16,1024]{1,0:T(8,128)(2,1)S(1)} %dynamic-slice_bitcast_fusion.2, bf16[4096,120]{0,1:T(8,128)(2,1)S(1)} %get-tuple-element.236, ...), kind=kOutput, calls=%fused_computation.10.clone.1 | convolution fusion | flops 3161907200 | bytes 13385733 | tf_op jit(solution)/shard_map/while/body/eval_jaxpr/pi,vpm->vim/dot_general | solution.py:39
  69.6 0.6 iota_compare_fusion.4
  70.2 10.9 %bitcast_add_fusion.2 = f32[16,120,800]{1,2,0:T(8,128)} fusion(f32[16,120,800]{1,2,0:T(8,128)} %get-tuple-element.224, pred[]{:T(512)S(6)} %compare.6, pred[1024,800]{0,1:T(8,128)(4,1)S(1)} %iota_compare_fusion.4, bf16[16,1024]{1,0:T(8,128)(2,1)S(1)} %dynamic-slice_bitcast_fusion.2, bf16[4096,120]{0,1:T(8,128)(2,1)S(1)} %get-tuple-element.236, ...), kind=kOutput, calls=%fused_computation.10.clone.1 | convolution fusion | flops 3161907200 | bytes 13385733 | tf_op jit(solution)/shard_map/while/body/eval_jaxpr/pi,vpm->vim/dot_general | solution.py:39
  81.1 0.9 copy-done.2
  82.0 0.1 copy.21
  82.1 5.4 %gather_fusion.1 = bf16[256,3072]{1,0:T(8,128)(2,1)S(1)} fusion(bf16[512,3072]{1,0:T(8,128)(2,1)} %all-gather.2.cloned.1.call-done, s32[1024]{0:T(1024)S(1)} %pad_clamp_fusion), kind=kCustom, calls=%fused_computation.3 | custom fusion | bytes 3146752 | tf_op jit(solution)/shard_map/jit(_take)/gather | solution.py:68
  87.6 0.6 fusion.19
  88.2 0.8 copy.25
  89.0 73.5 %reduce-scatter.2.cloned.1.call-done = f32[8,120,800]{1,2,0:T(8,128)} async-done(((f32[16,120,800]{1,2,0:T(8,128)}), f32[8,120,800]{1,2,0:T(8,128)}) %reduce-scatter.2.cloned.1.call-update) | async-done | bytes 3072016 | tf_op jit(solution)/shard_map/reduce_scatter | solution.py:79
  (32 shorter events, 0.3 us)
Async XLA Ops:
  8.0 10.8 %copy-start = (bf16[128,3072]{1,0:T(8,128)(2,1)S(1)}, bf16[128,3072]{1,0:T(8,128)(2,1)}, u32[]{:S(2)}) copy-start(bf16[128,3072]{1,0:T(8,128)(2,1)} %param.12) | copy-start | bytes 2359300
  8.0 13.9 %copy-start.1 = (bf16[800,120]{1,0:T(8,128)(2,1)S(1)}, bf16[800,120]{1,0:T(8,128)(2,1)}, u32[]{:S(2)}) copy-start(bf16[800,120]{1,0:T(8,128)(2,1)} %param.15) | copy-start | bytes 576004
  9.7 27.2 %all-to-all-start = ((bf16[128,16,16]{0,2,1:T(8,128)(2,1)}), bf16[128,16,16]{0,2,1:T(8,128)(2,1)S(1)}, u32[]{:S(2)}, u32[]{:S(2)}) async-start(bf16[128,16,16]{0,2,1:T(8,128)(2,1)} %bitcast.6), calls=%async_computation | async-start | bytes 131072 | tf_op jit(solution)/shard_map/all_to_all | solution.py:75
  17.1 65.0 %all-gather.2.cloned.1.call-start = ((), (), s32[]{:S(2)}) async-start(), calls=%async_computation.2 | async-start | bytes 3244032 | tf_op jit(solution)/shard_map/all_gather | solution.py:67
  20.2 142.2 %reduce-scatter.2.cloned.1.call-start = ((), (), s32[]{:S(2)}) async-start(), calls=%async_computation.3 | async-start | bytes 9830400 | tf_op jit(solution)/shard_map/reduce_scatter | solution.py:79
  81.1 0.9 copy-start.2
Sparse Core Ops, SparseCore 0:
  21.3 60.5 all-gather.1
Sparse Core Ops, SparseCore 1:
  81.2 81.2 reduce-scatter.1
where the time goes:
time: 170 us
  waiting for transfers between devices  73.5 us (43%)
  matrix products  42.2 us (25%)
  local copies, waits for them, and re-layouts  22.4 us (13%)
  between operations  15.7 us (9%)
  other arithmetic  8.4 us (5%)
  starting transfers between devices  7.47 us (4%)
    reduce_scatter x1, waiting for transfers between devices, per_device(): halves = lax.psum_scatter(partials, 'col', scatter_dimension=0, tiled=True)  73.5 us
    dot_general x4, matrix products, one_block(): jnp.einsum('pi,vpm->vim', coeff_block, spread, preferred_element_type=jnp...  41.6 us
    all_to_all x1, starting transfers between devices, per_device(): lax.all_to_all(grouped, 'row', split_axis=1, concat_axis=0, tiled=True)  7.39 us
    gather x1, local copies, waits for them, and re-layouts, half_transform(): jnp.take(occupied, second_ao, axis=0)  6.18 us
    gather x1, local copies, waits for them, and re-layouts, half_transform(): occ_first = jnp.take(occupied, first_ao, axis=0)  6.18 us
    gather x1, local copies, waits for them, and re-layouts, per_device(): pivot_rows = jnp.take(gathered, owner * slot_cap + earlier_count, axis=0)  5.45 us
    unnamed x11, local copies, waits for them, and re-layouts  3.94 us
  transfers between devices with their start and end apart: 3, of which 1 were waited for; matrix products, arithmetic and copies ran while one was open for 42% of the time, Pallas kernels for 0%

commit v1 on v0

v1 whole, which is shorter than its diff:
```python
import functools

import jax
import jax.numpy as jnp
from jax import lax
from jax.experimental import pallas as pl
from jax.experimental.pallas import tpu as pltpu
from jax.sharding import PartitionSpec as P

MESH = pl.DeviceIdType.MESH
LANES = 128
SUBL = 8


def exchange_kernel(
    row_count, col_count, depth,
    target_ref, fin_ref, slot_ref,
    rfin_ref, gat_ref,
    rslot, slot_send, slot_recv, fin_send, fin_recv,
    ag_recv, z_send, plane_send, core_send,
):
    devices = row_count * col_count
    r = lax.axis_index("row")
    c = lax.axis_index("col")
    me = r * col_count + c
    xs = 2
    zs = row_count // (2 * xs)
    core = r % 2
    x = (r // 2) % xs
    z = r // (2 * xs)

    def row_of(zz, xx, kk):
        return (zz * xs + xx) * 2 + kk

    def block_of(zz, xx, kk, yy):
        return row_of(zz, xx, kk) * col_count + yy

    barrier = pltpu.get_barrier_semaphore()

    def greet(k, carry):
        peer = (me + k) % devices
        pl.semaphore_signal(
            barrier, inc=1, device_id=(peer // col_count, peer % col_count), device_id_type=MESH
        )
        return carry

    lax.fori_loop(1, devices, greet, 0)
    pl.semaphore_wait(barrier, devices - 1)

    def slot_copy(peer, source):
        return pltpu.make_async_remote_copy(
            src_ref=slot_ref.at[peer], dst_ref=rslot.at[source],
            send_sem=slot_send.at[peer], recv_sem=slot_recv.at[source],
            device_id=(peer // col_count, peer % col_count), device_id_type=MESH,
        )

    def fin_copy(peer, source):
        return pltpu.make_async_remote_copy(
            src_ref=fin_ref.at[peer], dst_ref=rfin_ref.at[source],
            send_sem=fin_send.at[peer], recv_sem=fin_recv.at[source],
            device_id=(peer // col_count, peer % col_count), device_id_type=MESH,
        )

    def send_slot(k, carry):
        slot_copy((me + k) % devices, me).start()
        return carry

    def send_fin(k, carry):
        fin_copy((me + k) % devices, me).start()
        return carry

    lax.fori_loop(1, devices, send_slot, 0)
    lax.fori_loop(1, devices, send_fin, 0)
    rslot[me] = slot_ref[me]
    rfin_ref[me] = fin_ref[me]
    slot_total = rslot.shape[0] * rslot.shape[1]
    pivots = target_ref.shape[1]
    rows = lax.broadcasted_iota(jnp.int32, (slot_total, pivots), 0)
    one_hot = jnp.where(rows == target_ref[...], 1.0, 0.0).astype(jnp.bfloat16)

    def take_slot(k, carry):
        peer = (me + k) % devices
        slot_copy(peer, peer).wait_recv()
        return carry

    lax.fori_loop(1, devices, take_slot, 0)
    packed = lax.dot_general(
        rslot[...].reshape(slot_total, LANES), one_hot, (((0,), (0,)), ((), ())),
        preferred_element_type=jnp.float32,
    )
    gat_ref[me] = packed[:depth].astype(jnp.bfloat16)

    def block_copy(block, send_sem, zz, xx, kk, yy):
        return pltpu.make_async_remote_copy(
            src_ref=gat_ref.at[block], dst_ref=gat_ref.at[block],
            send_sem=send_sem, recv_sem=ag_recv.at[block],
            device_id=(row_of(zz, xx, kk), yy), device_id_type=MESH,
        )

    started = []

    def go(copy):
        copy.start()
        started.append(copy)

    plane = [(dx, dy) for dx in range(xs) for dy in range(col_count)]
    for dz in range(1, zs):
        go(block_copy(me, z_send.at[dz], (z + dz) % zs, x, core, c))
    for dz in range(zs):
        zz = (z + zs - dz) % zs
        block = block_of(zz, x, core, c)
        if dz > 0:
            block_copy(block, z_send.at[0], z, x, core, c).wait_recv()
        for dx, dy in plane[1:]:
            go(block_copy(
                block, plane_send.at[dz, dx * col_count + dy],
                z, (x + dx) % xs, core, (c + dy) % col_count,
            ))
        go(block_copy(block, core_send.at[dz, 0], z, x, 1 - core, c))
    for dz in range(zs):
        zz = (z + zs - dz) % zs
        for dx, dy in plane[1:]:
            block = block_of(zz, (x + dx) % xs, core, (c + dy) % col_count)
            block_copy(block, z_send.at[0], z, x, core, c).wait_recv()
            go(block_copy(
                block, core_send.at[dz, dx * col_count + dy], z, x, 1 - core, c
            ))

    def take_fin(k, carry):
        peer = (me + k) % devices
        fin_copy(peer, peer).wait_recv()
        fin_copy(peer, me).wait_send()
        slot_copy(peer, me).wait_send()
        return carry

    lax.fori_loop(1, devices, take_fin, 0)
    for dz in range(zs):
        zz = (z + zs - dz) % zs
        for dx, dy in plane:
            block = block_of(zz, (x + dx) % xs, 1 - core, (c + dy) % col_count)
            block_copy(block, z_send.at[0], z, x, core, c).wait_recv()
    for copy in started:
        copy.wait_send()


def exchange(mesh_shape, target, fin, slots, depth):
    row_count, col_count = mesh_shape
    devices = row_count * col_count
    zs = row_count // 4
    dma = pltpu.SemaphoreType.DMA
    vmem = pl.BlockSpec(memory_space=pltpu.VMEM)
    return pl.pallas_call(
        functools.partial(exchange_kernel, row_count, col_count, depth),
        out_shape=(
            jax.ShapeDtypeStruct(fin.shape, jnp.bfloat16),
            jax.ShapeDtypeStruct((devices, depth, target.shape[1]), jnp.bfloat16),
        ),
        in_specs=[vmem] * 3,
        out_specs=(vmem, vmem),
        scratch_shapes=[
            pltpu.VMEM(slots.shape, jnp.bfloat16),
            dma((devices,)), dma((devices,)), dma((devices,)), dma((devices,)),
            dma((devices,)), dma((zs,)), dma((zs, 2 * col_count)), dma((zs, 2 * col_count)),
        ],
        compiler_params=pltpu.CompilerParams(
            collective_id=0, has_side_effects=True, vmem_limit_bytes=40 * 1024 * 1024
        ),
        name="exchange",
    )(target, fin, slots)


def halves_kernel(orbitals, tiles, lower_ref, upper_ref, fin_ref, occ_ref, out_ref, mat):
    v = pl.program_id(0)
    stripe = orbitals * SUBL

    @pl.when(v == 0)
    def _():
        zero = jnp.zeros((40 * SUBL, LANES), jnp.float32)

        def clear(k, carry):
            mat[pl.ds(pl.multiple_of(k * 40 * SUBL, 8), 40 * SUBL), :] = zero
            return carry

        lax.fori_loop(0, tiles * orbitals // 40, clear, 0)
        lane = lax.broadcasted_iota(jnp.int32, (SUBL, LANES), 1)

        def spread(chunk, carry):
            values = fin_ref[chunk].astype(jnp.float32)
            for j in range(LANES):
                one = jnp.broadcast_to(values[:, j : j + 1], (SUBL, LANES))
                for place in (lower_ref, upper_ref):
                    word = place[chunk * LANES + j]
                    start = pl.multiple_of((word >> 7) * SUBL, SUBL)
                    pltpu.store(
                        mat.at[pl.ds(start, SUBL), :], one, mask=lane == (word & (LANES - 1))
                    )
            return carry

        lax.fori_loop(0, fin_ref.shape[0], spread, 0)

    for t in range(0, tiles, 2):
        parts = [
            mat[pl.ds(u * stripe + v, orbitals, stride=SUBL), :].astype(jnp.bfloat16)
            for u in range(t, min(t + 2, tiles))
        ]
        block = jnp.concatenate(parts, axis=1) if len(parts) > 1 else parts[0]
        low = t * LANES
        high = min(orbitals, low + block.shape[1])
        product = jnp.dot(occ_ref[...], block, preferred_element_type=jnp.float32)
        out_ref[0, :, low:high] = product[:, : high - low]


def half_transform(received, pairs, occupied, vectors):
    orbitals, occ = occupied.shape
    tiles = pl.cdiv(orbitals, LANES)
    first = pairs // orbitals
    second = pairs % orbitals

    def place(a, b):
        return (((b >> 7) * orbitals + a) << 7) | (b & (LANES - 1))

    smem = pl.BlockSpec(memory_space=pltpu.SMEM)
    vmem = pl.BlockSpec(memory_space=pltpu.VMEM)
    return pl.pallas_call(
        functools.partial(halves_kernel, orbitals, tiles),
        grid=(vectors,),
        out_shape=jax.ShapeDtypeStruct((vectors, occ, orbitals), jnp.float32),
        in_specs=[smem, smem, vmem, vmem],
        out_specs=pl.BlockSpec((1, occ, orbitals), lambda v: (v, 0, 0)),
        scratch_shapes=[pltpu.VMEM((tiles * orbitals * SUBL, LANES), jnp.float32)],
        compiler_params=pltpu.CompilerParams(vmem_limit_bytes=48 * 1024 * 1024),
        name="halves",
    )(place(first, second), place(second, first), received, occupied.T)


def per_device(mesh_shape, pivots, panel, prior, finished, pairs, occupied):
    rows_dev, width = prior.shape
    row_count, col_count = mesh_shape
    devices = row_count * col_count
    own_index = lax.axis_index("row") * col_count + lax.axis_index("col")
    piv_count = pivots.shape[0]
    slot_cap = max(16, 2 * piv_count // devices)
    owner = pivots // rows_dev
    counter = jnp.arange(piv_count, dtype=jnp.int32)
    earlier = (counter[None, :] < counter[:, None]) & (owner[None, :] == owner[:, None])
    rank = jnp.sum(earlier, axis=1).astype(jnp.int32)
    target = owner * slot_cap + rank
    wanted = target[None, :] == (
        own_index * slot_cap + jnp.arange(slot_cap, dtype=jnp.int32)
    )[:, None]
    local = jnp.sum(jnp.where(wanted, (pivots % rows_dev)[None, :], 0), axis=1)
    select = (
        local[:, None] == jnp.arange(rows_dev, dtype=jnp.int32)[None, :]
    ).astype(jnp.bfloat16)
    slot_rows = jnp.dot(select, prior, preferred_element_type=jnp.bfloat16)
    depth = width // devices
    slots = slot_rows.reshape(slot_cap, devices, depth).transpose(1, 0, 2)
    slots = jnp.pad(slots, ((0, 0), (0, 0), (0, LANES - depth)))
    vectors = finished.shape[1] // devices
    fin = finished.T.reshape(devices, vectors, rows_dev)
    fin = jnp.pad(fin, ((0, 0), (0, SUBL - vectors), (0, 0)))
    received, gathered = exchange(mesh_shape, target[None, :], fin, slots, depth)
    halves = half_transform(received, pairs, occupied, vectors)
    updated = panel - jnp.dot(
        prior, gathered.reshape(width, piv_count), preferred_element_type=jnp.float32
    )
    return (updated, halves)


def solution(mesh):
    mesh_shape = (mesh.shape["row"], mesh.shape["col"])
    return jax.shard_map(
        functools.partial(per_device, mesh_shape),
        mesh=mesh,
        in_specs=(
            P(),
            P(("row", "col"), None),
            P(("row", "col"), None),
            P(("row", "col"), None),
            P(),
            P(),
        ),
        out_specs=(P(("row", "col"), None), P(("row", "col"), None, None)),
        check_vma=False,
    )
```

time: 170 us -> 67.2 us (0.40)
  waiting for transfers between devices: 73.5 us -> 0 us
  Pallas kernels: 0 us -> 54.5 us
  matrix products: 42.2 us -> 0.86 us
  between operations: 15.7 us -> 0.78 us
  local copies, waits for them, and re-layouts: 22.4 us -> 8.78 us
  starting transfers between devices: 7.47 us -> 0 us
  other arithmetic: 8.4 us -> 1.93 us
    reduce_scatter x1 -> x0, waiting for transfers between devices: 73.5 us -> none  [per_device(): halves = lax.psum_scatter(partials, 'col', scatter_dimension=0, tiled=True)]
    pallas_call x0 -> x2, Pallas kernels: none -> 54.5 us  [the longest x1 28.9 us: exchange(): pl.pallas_call(functools.partial(exchange_kernel, row_count, col_count, d...]
    dot_general x5 -> x2, matrix products: 42.2 us -> 0.86 us  [the longest x1 0.6 us: per_device(): jnp.dot(prior, gathered.reshape(width, piv_count), preferred_element_type...]
    gather x4 -> x0, local copies, waits for them, and re-layouts: 18.4 us -> none  [the longest x1 6.18 us: half_transform(): jnp.take(occupied, second_ao, axis=0)]
    all_to_all x1 -> x0, starting transfers between devices: 7.39 us -> none  [per_device(): lax.all_to_all(grouped, 'row', split_axis=1, concat_axis=0, tiled=True)]
    unnamed x11 -> x12, local copies, waits for them, and re-layouts: 3.94 us -> 7.57 us
    eq x5 -> x0, other arithmetic: 3.07 us -> none  [the longest x4 2.38 us: one_block(): matches = target_block[:, None] == columns[None, :]]
    select_n x5 -> x1, other arithmetic: 3.21 us -> 0.81 us  [per_device(): local = jnp.sum(jnp.where(wanted, (pivots % rows_dev)[None, :], 0), axis=1)]
  transfers between devices with their start and end apart: 3 -> 0, of which waited for: 1 -> 0; matrix products, arithmetic and copies ran while one was open for 42% -> 0% of each run, Pallas kernels for 0% -> 0%
where the time goes in v1:
time: 67.2 us; the launch traced here: 66.9 us
  Pallas kernels  54.5 us (81%)
  local copies, waits for them, and re-layouts  8.78 us (13%)
  other arithmetic  1.93 us (3%)
  matrix products  0.86 us (1%)
  between operations  0.78 us (1%)
    pallas_call x1, Pallas kernels, exchange(): pl.pallas_call(functools.partial(exchange_kernel, row_count, col_count, d...  28.9 us
    pallas_call x1, Pallas kernels, half_transform(): pl.pallas_call(functools.partial(halves_kernel, orbitals, tiles), grid=(v...  25.6 us
    unnamed x12, local copies, waits for them, and re-layouts  7.57 us

profile of v1, /device:TPU:0, one launch (start us, length us, event | category | flops | bytes accessed | tf_op | source)
XLA Modules:
  0.0 66.9 jit_solution(7855737032110858252)
XLA Ops:
  0.6 0.0 copy-start
  0.6 0.0 copy-start.2
  0.7 0.0 copy-start.3
  0.7 0.8 %and_select_fusion = (s32[256]{0:T(256)S(1)}, s32[256]{0:T(256)S(1)}) fusion(s32[256]{0:T(256)} %param.6), kind=kLoop, calls=%fused_computation.17 | loop fusion | flops 4864 | bytes 3072 | tf_op jit(solution)/shard_map/jit(remainder)/select_n | solution.py:251
  1.5 0.2 convert_reduce_fusion
  1.7 0.2 select_reduce_fusion
  1.9 0.7 %and_or_fusion = (s32[4096]{0:T(1024)S(1)}, s32[4096]{0:T(1024)S(1)}) fusion(s32[4096]{0:T(1024)} %param.10), kind=kLoop, calls=%fused_computation.8 | loop fusion | flops 98304 | bytes 49152 | tf_op jit(solution)/shard_map/or | solution.py:220
  2.6 1.0 %copy.19 = bf16[256,128]{1,0:T(8,128)(2,1)S(1)} copy(bf16[256,128]{0,1:T(8,128)(2,1)} %bitcast.20) | data formatting | bytes 131072 | tf_op jit(solution)/shard_map/transpose | solution.py:260
  3.6 0.0 copy-done
  3.6 0.3 fusion.3
  3.8 0.2 reshape.23
  4.0 0.1 copy.26
  4.1 0.0 copy-done.3
  4.1 0.1 copy.21
  4.2 0.0 copy-done.2
  4.2 0.2 copy.22
  4.4 28.9 %exchange.1 = (bf16[32,8,128]{2,1,0:T(8,128)(2,1)S(1)}, bf16[32,96,256]{2,1,0:T(8,128)(2,1)S(1)}) custom-call(s32[1,256]{1,0:T(1,128)S(1)} %bitcast.18, bf16[32,8,128]{2,1,0:T(8,128)(2,1)S(1)} %bitcast.17, bf16[32,16,128]{2,1,0:T(8,128)(2,1)S(1)} %pad.4.slot_ref), custom_call_target="tpu_custom_call" | custom-call | tf_op jit(solution)/shard_map/exchange/pallas_call | solution.py:152
  33.3 0.6 fusion
  33.9 0.8 %copy.23 = f32[128,256]{1,0:T(8,128)} copy(f32[128,256]{0,1:T(8,128)S(1)} %fusion) | data formatting | bytes 262144
  34.7 25.6 %halves.1 = f32[8,120,800]{2,1,0:T(8,128)S(1)} custom-call(s32[4096]{0:T(1024)S(1)} %get-tuple-element.13.lower_ref, s32[4096]{0:T(1024)S(1)} %get-tuple-element.12.upper_ref, bf16[32,8,128]{2,1,0:T(8,128)(2,1)S(1)} %get-tuple-element.5.fin_ref, bf16[120,800]{1,0:T(8,128)(2,1)S(1)} %bitcast.16), custom_call_target="tpu_custom_call" | custom-call | tf_op jit(solution)/shard_map/halves/pallas_call | solution.py:224
  60.3 0.0 copy-start.1
  60.3 1.7 %copy-done.1 = f32[8,120,800]{2,1,0:T(8,128)} copy-done((f32[8,120,800]{2,1,0:T(8,128)}, f32[8,120,800]{2,1,0:T(8,128)S(1)}, u32[]{:S(2)}) %copy-start.1) | copy-done | bytes 3072024
  62.0 4.8 %copy.24 = f32[8,120,800]{1,2,0:T(8,128)} copy(f32[8,120,800]{2,1,0:T(8,128)} %copy-done.1) | data formatting | bytes 6144000
  (3 shorter events, 0.0 us)
Async XLA Ops:
  0.6 3.0 %copy-start = (bf16[128,3072]{1,0:T(8,128)(2,1)S(1)}, bf16[128,3072]{1,0:T(8,128)(2,1)}, u32[]{:S(2)}) copy-start(bf16[128,3072]{1,0:T(8,128)(2,1)} %param.8) | copy-start | bytes 2359300
  0.6 3.6 %copy-start.2 = (bf16[800,120]{1,0:T(8,128)(2,1)S(1)}, bf16[800,120]{1,0:T(8,128)(2,1)}, u32[]{:S(2)}) copy-start(bf16[800,120]{1,0:T(8,128)(2,1)} %param.11) | copy-start | bytes 576004
  0.7 3.5 %copy-start.3 = (f32[128,256]{1,0:T(8,128)S(1)}, f32[128,256]{1,0:T(8,128)}, u32[]{:S(2)}) copy-start(f32[128,256]{1,0:T(8,128)} %param.7) | copy-start | bytes 393220
  60.3 1.7 %copy-start.1 = (f32[8,120,800]{2,1,0:T(8,128)}, f32[8,120,800]{2,1,0:T(8,128)S(1)}, u32[]{:S(2)}) copy-start(f32[8,120,800]{2,1,0:T(8,128)S(1)} %halves.1) | copy-start | bytes 9216004

commit v2 on v1

v2 whole, which is shorter than its diff:
```python
import functools

import jax
import jax.numpy as jnp
from jax import lax
from jax.experimental import pallas as pl
from jax.experimental.pallas import tpu as pltpu
from jax.sharding import PartitionSpec as P

MESH = pl.DeviceIdType.MESH
LANES = 128
SUBL = 8


def exchange_kernel(
    row_count, col_count, depth,
    target_ref, local_ref, finished_ref, prior_ref,
    rfin_ref, gat_ref,
    prior_buf, fin_ref, slot_ref, rslot,
    load_sem, slot_send, slot_recv, fin_send, fin_recv,
    ag_recv, z_send, plane_send, core_send,
):
    devices = row_count * col_count
    r = lax.axis_index("row")
    c = lax.axis_index("col")
    me = r * col_count + c
    xs = 2
    zs = row_count // (2 * xs)
    core = r % 2
    x = (r // 2) % xs
    z = r // (2 * xs)

    def row_of(zz, xx, kk):
        return (zz * xs + xx) * 2 + kk

    def block_of(zz, xx, kk, yy):
        return row_of(zz, xx, kk) * col_count + yy

    def peer_of(k):
        return me ^ k if devices & (devices - 1) == 0 else (me + k) % devices

    def each_peer(body):
        if devices <= 64:
            for k in range(1, devices):
                body(peer_of(k))
        else:
            lax.fori_loop(1, devices, lambda k, carry: (body(peer_of(k)), carry)[1], 0)

    barrier = pltpu.get_barrier_semaphore()

    def greet(peer):
        pl.semaphore_signal(
            barrier, inc=1, device_id=(peer // col_count, peer % col_count), device_id_type=MESH
        )

    each_peer(greet)
    load = pltpu.make_async_copy(prior_ref, prior_buf, load_sem)
    load.start()
    target = target_ref[...]
    pivots = target.shape[1]
    slot_cap = slot_ref.shape[1]
    own_slots = me * slot_cap + lax.broadcasted_iota(jnp.int32, (slot_cap, pivots), 0)
    offsets = jnp.sum(
        jnp.where(own_slots == target, local_ref[...], 0.0), axis=1, keepdims=True
    ).astype(jnp.int32)
    rows_dev = prior_buf.shape[0]
    columns = lax.broadcasted_iota(jnp.int32, (slot_cap, rows_dev), 1)
    select = jnp.where(columns == offsets, 1.0, 0.0).astype(jnp.bfloat16)
    turned = finished_ref[...].astype(jnp.float32).T
    vectors = turned.shape[0] // devices
    if vectors < SUBL:
        fin_ref[...] = jnp.zeros_like(fin_ref)
    for d in range(devices):
        fin_ref[d, :vectors] = turned[d * vectors : (d + 1) * vectors].astype(jnp.bfloat16)
    load.wait()
    slot_rows = jnp.dot(
        select, prior_buf[...], preferred_element_type=jnp.float32
    )
    slot_ref[...] = jnp.zeros_like(slot_ref)
    for d in range(devices):
        slot_ref[d, :, :depth] = slot_rows[:, d * depth : (d + 1) * depth].astype(jnp.bfloat16)
    pl.semaphore_wait(barrier, devices - 1)

    def slot_copy(peer, source):
        return pltpu.make_async_remote_copy(
            src_ref=slot_ref.at[peer], dst_ref=rslot.at[source],
            send_sem=slot_send.at[peer], recv_sem=slot_recv.at[source],
            device_id=(peer // col_count, peer % col_count), device_id_type=MESH,
        )

    def fin_copy(peer, source):
        return pltpu.make_async_remote_copy(
            src_ref=fin_ref.at[peer], dst_ref=rfin_ref.at[source],
            send_sem=fin_send.at[peer], recv_sem=fin_recv.at[source],
            device_id=(peer // col_count, peer % col_count), device_id_type=MESH,
        )

    each_peer(lambda peer: slot_copy(peer, me).start())
    each_peer(lambda peer: fin_copy(peer, me).start())
    rslot[me] = slot_ref[me]
    rfin_ref[me] = fin_ref[me]
    slot_total = rslot.shape[0] * rslot.shape[1]
    rows = lax.broadcasted_iota(jnp.int32, (slot_total, pivots), 0)
    one_hot = jnp.where(rows == target, 1.0, 0.0).astype(jnp.bfloat16)

    each_peer(lambda peer: slot_copy(peer, peer).wait_recv())
    packed = lax.dot_general(
        rslot[...].reshape(slot_total, LANES), one_hot, (((0,), (0,)), ((), ())),
        preferred_element_type=jnp.float32,
    )
    gat_ref[me] = packed[:depth].astype(jnp.bfloat16)

    def block_copy(block, send_sem, zz, xx, kk, yy):
        return pltpu.make_async_remote_copy(
            src_ref=gat_ref.at[block], dst_ref=gat_ref.at[block],
            send_sem=send_sem, recv_sem=ag_recv.at[block],
            device_id=(row_of(zz, xx, kk), yy), device_id_type=MESH,
        )

    started = []

    def go(copy):
        copy.start()
        started.append(copy)

    plane = [(dx, dy) for dx in range(xs) for dy in range(col_count)]
    for dz in range(1, zs):
        go(block_copy(me, z_send.at[dz], (z + dz) % zs, x, core, c))
    for dz in range(zs):
        zz = (z + zs - dz) % zs
        block = block_of(zz, x, core, c)
        if dz > 0:
            block_copy(block, z_send.at[0], z, x, core, c).wait_recv()
        for dx, dy in plane[1:]:
            go(block_copy(
                block, plane_send.at[dz, dx * col_count + dy],
                z, (x + dx) % xs, core, (c + dy) % col_count,
            ))
        go(block_copy(block, core_send.at[dz, 0], z, x, 1 - core, c))
    for dz in range(zs):
        zz = (z + zs - dz) % zs
        for dx, dy in plane[1:]:
            block = block_of(zz, (x + dx) % xs, core, (c + dy) % col_count)
            block_copy(block, z_send.at[0], z, x, core, c).wait_recv()
            go(block_copy(
                block, core_send.at[dz, dx * col_count + dy], z, x, 1 - core, c
            ))

    def take_fin(peer):
        fin_copy(peer, peer).wait_recv()
        fin_copy(peer, me).wait_send()
        slot_copy(peer, me).wait_send()

    each_peer(take_fin)
    for dz in range(zs):
        zz = (z + zs - dz) % zs
        for dx, dy in plane:
            block = block_of(zz, (x + dx) % xs, 1 - core, (c + dy) % col_count)
            block_copy(block, z_send.at[0], z, x, core, c).wait_recv()
    for copy in started:
        copy.wait_send()


def exchange(mesh_shape, target, local, finished, prior, slot_cap):
    row_count, col_count = mesh_shape
    devices = row_count * col_count
    depth = prior.shape[1] // devices
    zs = row_count // 4
    dma = pltpu.SemaphoreType.DMA
    vmem = pl.BlockSpec(memory_space=pltpu.VMEM)
    fin_shape = (devices, SUBL, finished.shape[0])
    slot_shape = (devices, slot_cap, LANES)
    return pl.pallas_call(
        functools.partial(exchange_kernel, row_count, col_count, depth),
        out_shape=(
            jax.ShapeDtypeStruct(fin_shape, jnp.bfloat16),
            jax.ShapeDtypeStruct((devices, depth, target.shape[1]), jnp.bfloat16),
        ),
        in_specs=[vmem] * 3 + [pl.BlockSpec(memory_space=pl.ANY)],
        out_specs=(vmem, vmem),
        scratch_shapes=[
            pltpu.VMEM(prior.shape, jnp.bfloat16),
            pltpu.VMEM(fin_shape, jnp.bfloat16),
            pltpu.VMEM(slot_shape, jnp.bfloat16),
            pltpu.VMEM(slot_shape, jnp.bfloat16),
            dma, dma((devices,)), dma((devices,)), dma((devices,)), dma((devices,)),
            dma((devices,)), dma((zs,)), dma((zs, 2 * col_count)), dma((zs, 2 * col_count)),
        ],
        compiler_params=pltpu.CompilerParams(
            collective_id=0, has_side_effects=True, vmem_limit_bytes=40 * 1024 * 1024
        ),
        name="exchange",
    )(target, local, finished, prior)


def halves_kernel(
    orbitals, tiles, lower_ref, upper_ref, fin_ref, occ_ref, panel_ref, prior_ref, gat_ref,
    upd_ref, out_ref, mat,
):
    v = pl.program_id(0)
    stripe = orbitals * SUBL

    @pl.when(v == 0)
    def _():
        upd_ref[...] = panel_ref[...] - jnp.dot(
            prior_ref[...], gat_ref[...], preferred_element_type=jnp.float32
        )
        zero = jnp.zeros((40 * SUBL, LANES), jnp.float32)

        def clear(k, carry):
            mat[pl.ds(pl.multiple_of(k * 40 * SUBL, 8), 40 * SUBL), :] = zero
            return carry

        lax.fori_loop(0, tiles * orbitals // 40, clear, 0)
        lane = lax.broadcasted_iota(jnp.int32, (SUBL, LANES), 1)

        def spread(chunk, carry):
            values = fin_ref[chunk].astype(jnp.float32)
            for j in range(LANES):
                one = jnp.broadcast_to(values[:, j : j + 1], (SUBL, LANES))
                for place in (lower_ref, upper_ref):
                    word = place[chunk * LANES + j]
                    start = pl.multiple_of(word >> 7, SUBL)
                    here = (jnp.full((SUBL, LANES), word) & (LANES - 1)) == lane
                    pltpu.store(mat.at[pl.ds(start, SUBL), :], one, mask=here)
            return carry

        lax.fori_loop(0, fin_ref.shape[0], spread, 0)

    block = jnp.concatenate(
        [
            mat[pl.ds(t * stripe + v, orbitals, stride=SUBL), :].astype(jnp.bfloat16)
            for t in range(tiles)
        ],
        axis=1,
    )[:, :orbitals]
    out_ref[0] = jnp.dot(block, occ_ref[...], preferred_element_type=jnp.float32)


def finish(received, pairs, occupied, panel, prior, gathered, vectors):
    orbitals, occ = occupied.shape
    tiles = pl.cdiv(orbitals, LANES)
    first = pairs // orbitals
    second = pairs % orbitals

    def place(a, b):
        return (((b >> 7) * orbitals + a) << 10) | (b & (LANES - 1))

    smem = pl.BlockSpec(memory_space=pltpu.SMEM)
    vmem = pl.BlockSpec(memory_space=pltpu.VMEM)
    updated, halves = pl.pallas_call(
        functools.partial(halves_kernel, orbitals, tiles),
        grid=(vectors,),
        out_shape=(
            jax.ShapeDtypeStruct(panel.shape, jnp.float32),
            jax.ShapeDtypeStruct((vectors, orbitals, occ), jnp.float32),
        ),
        in_specs=[smem, smem] + [vmem] * 5,
        out_specs=(
            pl.BlockSpec(panel.shape, lambda v: (0, 0)),
            pl.BlockSpec((1, orbitals, occ), lambda v: (v, 0, 0)),
        ),
        scratch_shapes=[pltpu.VMEM((tiles * orbitals * SUBL, LANES), jnp.float32)],
        compiler_params=pltpu.CompilerParams(vmem_limit_bytes=48 * 1024 * 1024),
        name="halves",
    )(
        place(first, second), place(second, first), received,
        occupied, panel, prior, gathered,
    )
    return updated, halves.transpose(0, 2, 1)


def per_device(mesh_shape, pivots, panel, prior, finished, pairs, occupied):
    rows_dev, width = prior.shape
    row_count, col_count = mesh_shape
    devices = row_count * col_count
    piv_count = pivots.shape[0]
    slot_cap = max(16, 2 * piv_count // devices)
    owner = pivots // rows_dev
    counter = jnp.arange(piv_count, dtype=jnp.int32)
    earlier = (counter[None, :] < counter[:, None]) & (owner[None, :] == owner[:, None])
    rank = jnp.sum(earlier, axis=1).astype(jnp.int32)
    target = owner * slot_cap + rank
    vectors = finished.shape[1] // devices
    local = (pivots % rows_dev).astype(jnp.float32)
    received, gathered = exchange(
        mesh_shape, target[None, :], local[None, :], finished, prior, slot_cap
    )
    return finish(
        received, pairs, occupied, panel, prior, gathered.reshape(width, piv_count), vectors
    )


def solution(mesh):
    mesh_shape = (mesh.shape["row"], mesh.shape["col"])
    return jax.shard_map(
        functools.partial(per_device, mesh_shape),
        mesh=mesh,
        in_specs=(
            P(),
            P(("row", "col"), None),
            P(("row", "col"), None),
            P(("row", "col"), None),
            P(),
            P(),
        ),
        out_specs=(P(("row", "col"), None), P(("row", "col"), None, None)),
        check_vma=False,
    )
```

time: 67.2 us -> 57.3 us (0.85)
  Pallas kernels: 54.5 us -> 49.7 us
  local copies, waits for them, and re-layouts: 8.78 us -> 4.93 us
  matrix products: 0.86 us -> 0 us
    pallas_call x1, Pallas kernels: 25.6 us -> 21 us  [finish(): pl.pallas_call(functools.partial(halves_kernel, orbitals, tiles), grid=(v...]
    unnamed x12 -> x10, local copies, waits for them, and re-layouts: 7.57 us -> 4.93 us
    transpose x1 -> x0, local copies, waits for them, and re-layouts: 0.95 us -> none  [per_device(): fin = finished.T.reshape(devices, vectors, rows_dev)]
    dot_general x2 -> x0, matrix products: 0.86 us -> none  [the longest x1 0.6 us: per_device(): jnp.dot(prior, gathered.reshape(width, piv_count), preferred_element_type...]
    select_n x1 -> x0, other arithmetic: 0.81 us -> none  [per_device(): local = jnp.sum(jnp.where(wanted, (pivots % rows_dev)[None, :], 0), axis=1)]
    convert_element_type x0 -> x1, other arithmetic: none -> 0.69 us  [per_device(): local = (pivots % rows_dev).astype(jnp.float32)]
where the time goes in v2:
time: 57.3 us; the launch traced here: 56.9 us
  Pallas kernels  49.7 us (87%)
  local copies, waits for them, and re-layouts  4.93 us (9%)
  other arithmetic  1.63 us (3%)
  between operations  0.67 us (1%)
    pallas_call x1, Pallas kernels, exchange(): pl.pallas_call(functools.partial(exchange_kernel, row_count, col_count, d...  28.7 us
    pallas_call x1, Pallas kernels, finish(): pl.pallas_call(functools.partial(halves_kernel, orbitals, tiles), grid=(v...  21 us
    unnamed x10, local copies, waits for them, and re-layouts  4.93 us

profile of v2, /device:TPU:0, one launch (start us, length us, event | category | flops | bytes accessed | tf_op | source)
XLA Modules:
  0.0 56.9 jit_solution(17676764574107763378)
XLA Ops:
  0.6 0.7 %fusion.2 = (f32[256]{0:T(256)S(1)}, s32[256]{0:T(256)S(1)}) fusion(s32[256]{0:T(256)} %param.6), kind=kLoop, calls=%fused_computation.15 | loop fusion | flops 5120 | bytes 3072 | tf_op jit(solution)/shard_map/convert_element_type | solution.py:285
  1.3 0.2 convert_reduce_fusion
  1.5 0.7 %and_or_fusion = (s32[4096]{0:T(1024)S(1)}, s32[4096]{0:T(1024)S(1)}) fusion(s32[4096]{0:T(1024)} %param.10), kind=kLoop, calls=%fused_computation.5 | loop fusion | flops 98304 | bytes 49152 | tf_op jit(solution)/shard_map/or | solution.py:247
  2.3 0.0 copy-start
  2.3 1.1 %copy-done = bf16[128,3072]{1,0:T(8,128)(2,1)S(1)} copy-done((bf16[128,3072]{1,0:T(8,128)(2,1)S(1)}, bf16[128,3072]{1,0:T(8,128)(2,1)}, u32[]{:S(2)}) %copy-start) | copy-done | bytes 786456
  3.4 0.0 copy-start.4
  3.4 0.8 %copy-done.4 = bf16[128,256]{1,0:T(8,128)(2,1)S(1)} copy-done((bf16[128,256]{1,0:T(8,128)(2,1)S(1)}, bf16[128,256]{1,0:T(8,128)(2,1)}, u32[]{:S(2)}) %copy-start.4) | copy-done | bytes 65560
  4.2 28.7 %exchange.1 = (bf16[32,8,128]{2,1,0:T(8,128)(2,1)S(1)}, bf16[32,96,256]{2,1,0:T(8,128)(2,1)S(1)}) custom-call(s32[1,256]{1,0:T(1,128)S(1)} %bitcast.6, f32[1,256]{1,0:T(1,128)S(1)} %bitcast.5, bf16[128,256]{1,0:T(8,128)(2,1)S(1)} %copy-done.4, bf16[128,3072]{1,0:T(8,128)(2,1)S(1)} %copy-done), custom_call_target="tpu_custom_call" | custom-call | tf_op jit(solution)/shard_map/exchange/pallas_call | solution.py:173
  33.0 0.0 copy-start.1
  33.0 1.1 %copy-done.1 = bf16[128,3072]{1,0:T(8,128)(2,1)S(1)} copy-done((bf16[128,3072]{1,0:T(8,128)(2,1)S(1)}, bf16[128,3072]{1,0:T(8,128)(2,1)}, u32[]{:S(2)}) %copy-start.1) | copy-done | bytes 786456
  34.1 0.0 copy-start.2
  34.1 0.9 %copy-done.2 = bf16[800,120]{1,0:T(8,128)(2,1)S(1)} copy-done((bf16[800,120]{1,0:T(8,128)(2,1)S(1)}, bf16[800,120]{1,0:T(8,128)(2,1)}, u32[]{:S(2)}) %copy-start.2) | copy-done | bytes 192024
  35.0 0.0 copy-start.3
  35.0 0.9 %copy-done.3 = f32[128,256]{1,0:T(8,128)S(1)} copy-done((f32[128,256]{1,0:T(8,128)S(1)}, f32[128,256]{1,0:T(8,128)}, u32[]{:S(2)}) %copy-start.3) | copy-done | bytes 131096
  35.9 21.0 %halves.1 = (f32[128,256]{1,0:T(8,128)}, f32[8,800,120]{2,1,0:T(8,128)}) custom-call(s32[4096]{0:T(1024)S(1)} %get-tuple-element.11.lower_ref, s32[4096]{0:T(1024)S(1)} %get-tuple-element.10.upper_ref, bf16[32,8,128]{2,1,0:T(8,128)(2,1)S(1)} %get-tuple-element.6.fin_ref, bf16[800,120]{1,0:T(8,128)(2,1)S(1)} %copy-done.2, f32[128,256]{1,0:T(8,128)S(1)} %copy-done.3, ...), custom_call_target="tpu_custom_call" | custom-call | tf_op jit(solution)/shard_map/halves/pallas_call | solution.py:251
  (1 shorter events, 0.0 us)
Async XLA Ops:
  2.3 1.1 %copy-start = (bf16[128,3072]{1,0:T(8,128)(2,1)S(1)}, bf16[128,3072]{1,0:T(8,128)(2,1)}, u32[]{:S(2)}) copy-start(bf16[128,3072]{1,0:T(8,128)(2,1)} %prior_ref.3) | copy-start | bytes 2359300
  3.4 0.8 %copy-start.4 = (bf16[128,256]{1,0:T(8,128)(2,1)S(1)}, bf16[128,256]{1,0:T(8,128)(2,1)}, u32[]{:S(2)}) copy-start(bf16[128,256]{1,0:T(8,128)(2,1)} %finished_ref.1) | copy-start | bytes 196612
  33.0 1.1 %copy-start.1 = (bf16[128,3072]{1,0:T(8,128)(2,1)S(1)}, bf16[128,3072]{1,0:T(8,128)(2,1)}, u32[]{:S(2)}) copy-start(bf16[128,3072]{1,0:T(8,128)(2,1)} %prior_ref.3) | copy-start | bytes 2359300
  34.1 0.9 %copy-start.2 = (bf16[800,120]{1,0:T(8,128)(2,1)S(1)}, bf16[800,120]{1,0:T(8,128)(2,1)}, u32[]{:S(2)}) copy-start(bf16[800,120]{1,0:T(8,128)(2,1)} %occ_ref.1) | copy-start | bytes 576004
  35.0 0.9 %copy-start.3 = (f32[128,256]{1,0:T(8,128)S(1)}, f32[128,256]{1,0:T(8,128)}, u32[]{:S(2)}) copy-start(f32[128,256]{1,0:T(8,128)} %panel_ref.1) | copy-start | bytes 393220

commit v3 on v2

--- a/solution.py
+++ b/solution.py
@@ -189,6 +189,7 @@
         compiler_params=pltpu.CompilerParams(
             collective_id=0, has_side_effects=True, vmem_limit_bytes=40 * 1024 * 1024
         ),
+        cost_estimate=pl.CostEstimate(flops=10**10, bytes_accessed=4 * 10**7, transcendentals=0),
         name="exchange",
     )(target, local, finished, prior)
 
@@ -262,6 +263,7 @@
         ),
         scratch_shapes=[pltpu.VMEM((tiles * orbitals * SUBL, LANES), jnp.float32)],
         compiler_params=pltpu.CompilerParams(vmem_limit_bytes=48 * 1024 * 1024),
+        cost_estimate=pl.CostEstimate(flops=10**10, bytes_accessed=4 * 10**7, transcendentals=0),
         name="halves",
     )(
         place(first, second), place(second, first), received,

time: 57.3 us -> 54.5 us (0.951)
  local copies, waits for them, and re-layouts: 4.93 us -> 1.98 us
    unnamed x10, local copies, waits for them, and re-layouts: 4.93 us -> 1.98 us
where the time goes in v3:
time: 54.5 us; the launch traced here: 54.2 us
  Pallas kernels  49.9 us (92%)
  local copies, waits for them, and re-layouts  1.98 us (4%)
  other arithmetic  1.63 us (3%)
  between operations  0.69 us (1%)
    pallas_call x1, Pallas kernels, exchange(): pl.pallas_call(functools.partial(exchange_kernel, row_count, col_count, d...  28.9 us
    pallas_call x1, Pallas kernels, finish(): pl.pallas_call(functools.partial(halves_kernel, orbitals, tiles), grid=(v...  21 us
    unnamed x10, local copies, waits for them, and re-layouts  1.98 us

profile of v3, /device:TPU:0, one launch (start us, length us, event | category | flops | bytes accessed | tf_op | source)
XLA Modules:
  0.0 54.2 jit_solution(16621032089364560453)
XLA Ops:
  0.6 0.7 %fusion.2 = (f32[256]{0:T(256)S(1)}, s32[256]{0:T(256)S(1)}) fusion(s32[256]{0:T(256)} %param.6), kind=kLoop, calls=%fused_computation.15 | loop fusion | flops 5120 | bytes 3072 | tf_op jit(solution)/shard_map/convert_element_type | solution.py:287
  1.3 0.2 convert_reduce_fusion
  1.5 0.7 %and_or_fusion = (s32[4096]{0:T(1024)S(1)}, s32[4096]{0:T(1024)S(1)}) fusion(s32[4096]{0:T(1024)} %param.10), kind=kLoop, calls=%fused_computation.5 | loop fusion | flops 98304 | bytes 49152 | tf_op jit(solution)/shard_map/or | solution.py:248
  2.3 0.0 copy-start
  2.3 1.1 %copy-done = bf16[128,3072]{1,0:T(8,128)(2,1)S(1)} copy-done((bf16[128,3072]{1,0:T(8,128)(2,1)S(1)}, bf16[128,3072]{1,0:T(8,128)(2,1)}, u32[]{:S(2)}) %copy-start) | copy-done | bytes 786456
  3.4 0.0 copy-start.4
  3.4 0.8 %copy-done.4 = bf16[128,256]{1,0:T(8,128)(2,1)S(1)} copy-done((bf16[128,256]{1,0:T(8,128)(2,1)S(1)}, bf16[128,256]{1,0:T(8,128)(2,1)}, u32[]{:S(2)}) %copy-start.4) | copy-done | bytes 65560
  4.2 0.0 copy-start.1
  4.2 0.0 copy-start.2
  4.2 0.0 copy-start.3
  4.3 28.9 %exchange.1 = (bf16[32,8,128]{2,1,0:T(8,128)(2,1)S(1)}, bf16[32,96,256]{2,1,0:T(8,128)(2,1)S(1)}) custom-call(s32[1,256]{1,0:T(1,128)S(1)} %bitcast.5, f32[1,256]{1,0:T(1,128)S(1)} %bitcast.4, bf16[128,256]{1,0:T(8,128)(2,1)S(1)} %copy-done.4, bf16[128,3072]{1,0:T(8,128)(2,1)S(1)} %copy-done), custom_call_target="tpu_custom_call" | custom-call | flops 10000000000 | bytes 40000000 | tf_op jit(solution)/shard_map/exchange/pallas_call | solution.py:173
  33.2 0.0 copy-done.1
  33.2 0.0 copy-done.2
  33.2 0.0 copy-done.3
  33.2 21.0 %halves.1 = (f32[128,256]{1,0:T(8,128)}, f32[8,800,120]{2,1,0:T(8,128)}) custom-call(s32[4096]{0:T(1024)S(1)} %get-tuple-element.11.lower_ref, s32[4096]{0:T(1024)S(1)} %get-tuple-element.10.upper_ref, bf16[32,8,128]{2,1,0:T(8,128)(2,1)S(1)} %get-tuple-element.6.fin_ref, bf16[800,120]{1,0:T(8,128)(2,1)S(1)} %copy-done.2, f32[128,256]{1,0:T(8,128)S(1)} %copy-done.3, ...), custom_call_target="tpu_custom_call" | custom-call | flops 10000000000 | bytes 40000000 | tf_op jit(solution)/shard_map/halves/pallas_call | solution.py:252
  (1 shorter events, 0.0 us)
Async XLA Ops:
  2.3 1.1 %copy-start = (bf16[128,3072]{1,0:T(8,128)(2,1)S(1)}, bf16[128,3072]{1,0:T(8,128)(2,1)}, u32[]{:S(2)}) copy-start(bf16[128,3072]{1,0:T(8,128)(2,1)} %prior_ref.3) | copy-start | bytes 2359300
  3.4 0.8 %copy-start.4 = (bf16[128,256]{1,0:T(8,128)(2,1)S(1)}, bf16[128,256]{1,0:T(8,128)(2,1)}, u32[]{:S(2)}) copy-start(bf16[128,256]{1,0:T(8,128)(2,1)} %finished_ref.1) | copy-start | bytes 196612
  4.2 28.9 %copy-start.1 = (bf16[128,3072]{1,0:T(8,128)(2,1)S(1)}, bf16[128,3072]{1,0:T(8,128)(2,1)}, u32[]{:S(2)}) copy-start(bf16[128,3072]{1,0:T(8,128)(2,1)} %prior_ref.3) | copy-start | bytes 2359300
  4.2 28.9 %copy-start.2 = (bf16[800,120]{1,0:T(8,128)(2,1)S(1)}, bf16[800,120]{1,0:T(8,128)(2,1)}, u32[]{:S(2)}) copy-start(bf16[800,120]{1,0:T(8,128)(2,1)} %occ_ref.1) | copy-start | bytes 576004
  4.2 28.9 %copy-start.3 = (f32[128,256]{1,0:T(8,128)S(1)}, f32[128,256]{1,0:T(8,128)}, u32[]{:S(2)}) copy-start(f32[128,256]{1,0:T(8,128)} %panel_ref.1) | copy-start | bytes 393220
